TPU v7x, 32 devices: a whole 2x2x4 slice. The times are simulated.
32 devices in a mesh: lvl: 8 (over z, y), lon: 4 (over x, core).
Axes of the slice: x: 2, y: 2, z: 4, core: 2. Of those that a mesh axis runs over, the one named last changes fastest.
Arguments:
- window: float32 [8, 16, 69, 512], P('lvl', None, None, 'lon'), may hold values from -6 to 6
- anchor: float32 [16, 69, 512], P(None, None, 'lon'), may hold values from -6 to 6
- noise: float32 [8, 16, 69, 512], P('lvl', None, None, 'lon'), may hold values from -6 to 6
- conv_in: bfloat16 [3, 3, 192, 69], replicated, may hold values from -0.25 to 0.25
- conv_out: bfloat16 [3, 3, 69, 192], replicated, may hold values from -0.15625 to 0.15625
- time_shift: float32 [192], replicated, may hold values from -4 to 4
- plan: int32 [256], replicated, may hold values from 0 to 999, as said below
- start: int32 [1], replicated, may hold values from 0 to 247
Outputs:
- advanced: float32 [8, 16, 69, 512], P('lvl', None, None, 'lon')
Inputs may be any that keep to these rules, and one draw needn't show every extreme that they name: `plan`: strictly decreasing, first entry 999.
All inputs are finite; a program needn't handle non-finite values.
Results may differ from a plain program's by a relative error of at most 0.0003.
Values may be sent and summed in bfloat16 or wider, within the bound.
No kernel may reach another device: no remote copies, remote signals or barrier semaphores. Data moves between devices by JAX's collectives and lax.ppermute only.
A program may use at most 64 MiB of HBM per device.

v0:
```python
import jax
import jax.numpy as jnp
from jax import lax
from jax.sharding import PartitionSpec as P

SWEEPS = 2


def extended(block, sides, width):
    for axis, dim in sides:
        count = lax.axis_size(axis)
        forward = [(i, i + 1) for i in range(count - 1)]
        forward.append((count - 1, 0))
        backward = [(target, source) for source, target in forward]
        low = lax.ppermute(
            lax.slice_in_dim(block, block.shape[dim] - width, None, axis=dim), axis, forward
        )
        high = lax.ppermute(lax.slice_in_dim(block, 0, width, axis=dim), axis, backward)
        block = jnp.concatenate([low, block, high], axis=dim)
    return block


def convolve(padded, weight, width_out):
    rows = padded.shape[1] - 2
    total = jnp.zeros((padded.shape[0], rows, weight.shape[2], width_out), jnp.float32)
    for a in range(3):
        for b in range(3):
            piece = padded[:, a : a + rows, :, b : b + width_out]
            total = total + jnp.einsum(
                "oc,vlcn->vlon", weight[a, b], piece, preferred_element_type=jnp.float32
            )
    return total


def pad_rows(field):
    return jnp.pad(field, ((0, 0), (1, 1), (0, 0), (0, 0)))


def exclusive_sum(values):
    running = jnp.cumsum(values, axis=0)
    return jnp.concatenate([jnp.zeros_like(values[:1]), running[:-1]], axis=0)


def body(window, anchor, noise, conv_in, conv_out, time_shift, plan, start):
    levels_here = window.shape[0]
    width = window.shape[3]
    offset = start[0] + lax.axis_index("lvl") * levels_here
    times = lax.dynamic_slice(plan, (offset,), (levels_here + 1,)).astype(jnp.float32)
    t_now = times[:-1]
    beta = 0.1 + 19.9 * t_now / 1000.0
    step = (t_now - times[1:]) / 1000.0
    beta_col = beta[:, None, None, None]
    step_col = step[:, None, None, None]
    spread = jnp.sqrt(beta * step)[:, None, None, None] * noise
    shift = (t_now / 1000.0)[:, None, None, None] * time_shift[None, None, :, None]
    states = window
    inclusive = None
    for sweep in range(SWEEPS):
        rounded = states.astype(jnp.bfloat16)
        rimmed = extended(rounded, (("lon", 3),), 1)
        pre = convolve(pad_rows(rimmed), conv_in, width)
        hidden = jax.nn.silu(pre + shift).astype(jnp.bfloat16)
        hidden_wide = extended(hidden, (("lon", 3),), 1)
        score = convolve(pad_rows(hidden_wide), conv_out, width)
        increment = (0.5 * beta_col * states + beta_col * score) * step_col + spread
        earlier = exclusive_sum(
            lax.all_to_all(increment, "lvl", split_axis=1, concat_axis=0, tiled=True)
        )
        before = lax.all_to_all(earlier, "lvl", split_axis=0, concat_axis=1, tiled=True)
        inclusive = before + increment
        states = anchor[None] + before
    return anchor[None] + inclusive


def solution(mesh):
    return jax.shard_map(
        body,
        mesh=mesh,
        in_specs=(
            P("lvl", None, None, "lon"),
            P(None, None, "lon"),
            P("lvl", None, None, "lon"),
            P(),
            P(),
            P(),
            P(),
            P(),
        ),
        out_specs=P("lvl", None, None, "lon"),
        check_vma=False,
    )
```

profile of v0, /device:TPU:0, one launch (start us, length us, event | category | flops | bytes accessed | tf_op | source)
XLA Modules:
  0.0 134.5 jit_solution(6368105280167487864)
XLA Ops:
  0.0 1.3 copy.76
  1.5 0.5 collective-permute-start
  2.0 2.0 %collective-permute-start.1 = (bf16[1,16,69,1]{3,2,1,0:T(8,128)(2,1)S(1)}, bf16[1,16,69,1]{3,2,1,0:T(8,128)(2,1)S(1)}, u32[]{:S(2)}, u32[]{:S(2)}) collective-permute-start(bf16[1,16,69,1]{3,2,1,0:T(8,128)(2,1)S(1)} %get-tuple-element.14), channel_id=1, source_target_pairs={{1,0},{2,1},{3,2},{0,3},{5,4},{6,5},{7,6},{4,7},{9,8},{10,9},{11,1... | collective-permute-start | bytes 6632 | tf_op jit(solution)/shard_map/ppermute | solution.py:18
  4.7 0.6 fusion.153
  5.3 0.4 fusion.65
  6.4 2.4 %collective-permute-done = bf16[1,16,69,1]{3,2,1,0:T(8,128)(2,1)S(1)} collective-permute-done((bf16[1,16,69,1]{3,2,1,0:T(8,128)(2,1)S(1)}, bf16[1,16,69,1]{3,2,1,0:T(8,128)(2,1)S(1)}, u32[]{:S(2)}, u32[]{:S(2)}) %collective-permute-start) | collective-permute-done | bytes 2240 | tf_op jit(solution)/shard_map/ppermute | solution.py:15
  8.9 2.4 %collective-permute-done.1 = bf16[1,16,69,1]{3,2,1,0:T(8,128)(2,1)S(1)} collective-permute-done((bf16[1,16,69,1]{3,2,1,0:T(8,128)(2,1)S(1)}, bf16[1,16,69,1]{3,2,1,0:T(8,128)(2,1)S(1)}, u32[]{:S(2)}, u32[]{:S(2)}) %collective-permute-start.1) | collective-permute-done | bytes 2240 | tf_op jit(solution)/shard_map/ppermute | solution.py:18
  11.3 0.4 select_maximum_fusion.6
  11.7 0.5 fusion.53
  12.2 0.4 fusion.54
  12.6 0.5 fusion.62
  13.0 0.5 fusion.63
  13.5 0.4 fusion.64
  13.9 0.5 fusion.52
  14.4 0.5 fusion.59
  14.9 1.2 fusion.8
  16.1 0.3 fusion.150
  16.4 0.4 copy.42
  16.8 0.4 copy.43
  17.2 2.3 %collective-permute-start.3 = (bf16[1,16,192,1]{2,1,3,0:T(8,128)(2,1)S(1)}, bf16[1,16,192,1]{2,1,3,0:T(8,128)(2,1)S(1)}, u32[]{:S(2)}, u32[]{:S(2)}) collective-permute-start(bf16[1,16,192,1]{2,1,3,0:T(8,128)(2,1)S(1)} %copy.43), channel_id=1, source_target_pairs={{1,0},{2,1},{3,2},{0,3},{5,4},{6,5},{7,6},{4,7},{9,8},{10,9},{11,1... | collective-permute-start | bytes 18440 | tf_op jit(solution)/shard_map/ppermute | solution.py:18
  21.6 0.4 copy.44
  22.0 0.4 copy.45
  22.5 0.9 select_maximum_fusion.2
  23.5 0.5 fusion.34
  24.2 0.5 convolution_add_fusion.14
  24.7 0.5 convolution_add_fusion.13
  25.5 0.7 convolution_add_fusion.11
  26.5 0.5 convolution_add_fusion.9
  26.9 0.3 copy-done
  27.4 0.6 fusion.17
  28.1 0.6 copy.49
  28.6 22.1 %all_to_all.48 = f32[1,16,69,128]{3,0,2,1:T(1,128)S(1)} all-to-all(f32[1,16,69,128]{3,0,2,1:T(1,128)S(1)} %copy.49), channel_id=1, replica_groups=mesh['lvl'=8,'lon'=4] {'lvl'}, dimensions={1} | all-to-all | bytes 1130496 | tf_op jit(solution)/shard_map/all_to_all | solution.py:67
  51.4 18.8 %all_to_all.49 = f32[8,2,69,128]{3,1,2,0:T(2,128)S(1)} all-to-all(f32[8,2,69,128]{3,1,2,0:T(2,128)S(1)} %concatenate.48.clone), channel_id=1, replica_groups=mesh['lvl'=8,'lon'=4] {'lvl'}, dimensions={0} | all-to-all | bytes 1130496 | tf_op jit(solution)/shard_map/all_to_all | solution.py:69
  70.7 1.7 %collective-permute-start.5 = (bf16[1,16,69,1]{3,2,1,0:T(8,128)(2,1)S(1)}, bf16[1,16,69,1]{3,2,1,0:T(8,128)(2,1)S(1)}, u32[]{:S(2)}, u32[]{:S(2)}) collective-permute-start(bf16[1,16,69,1]{3,2,1,0:T(8,128)(2,1)S(1)} %get-tuple-element.12), channel_id=1, source_target_pairs={{1,0},{2,1},{3,2},{0,3},{5,4},{6,5},{7,6},{4,7},{9,8},{10,9},{11,1... | collective-permute-start | bytes 6632 | tf_op jit(solution)/shard_map/ppermute | solution.py:18
  72.5 0.4 fusion.67
  72.9 6.7 %collective-permute-done.4 = bf16[1,16,69,1]{3,2,1,0:T(8,128)(2,1)S(1)} collective-permute-done((bf16[1,16,69,1]{3,2,1,0:T(8,128)(2,1)S(1)}, bf16[1,16,69,1]{3,2,1,0:T(8,128)(2,1)S(1)}, u32[]{:S(2)}, u32[]{:S(2)}) %collective-permute-start.4) | collective-permute-done | bytes 2240 | tf_op jit(solution)/shard_map/ppermute | solution.py:15
  79.5 0.4 select_maximum_fusion.4
  79.9 0.5 fusion.40
  80.4 0.4 fusion.41
  80.8 0.5 fusion.49
  81.3 0.5 fusion.50
  81.8 0.4 fusion.51
  82.2 0.5 fusion.39
  82.6 0.5 fusion.46
  83.1 1.2 fusion.9
  84.3 0.3 fusion.149
  84.6 0.4 copy.54
  85.0 0.3 collective-permute-start.6
  85.3 0.4 copy.55
  85.7 1.5 %collective-permute-start.7 = (bf16[1,16,192,1]{2,1,3,0:T(8,128)(2,1)S(1)}, bf16[1,16,192,1]{2,1,3,0:T(8,128)(2,1)S(1)}, u32[]{:S(2)}, u32[]{:S(2)}) collective-permute-start(bf16[1,16,192,1]{2,1,3,0:T(8,128)(2,1)S(1)} %copy.55), channel_id=1, source_target_pairs={{1,0},{2,1},{3,2},{0,3},{5,4},{6,5},{7,6},{4,7},{9,8},{10,9},{11,1... | collective-permute-start | bytes 18440 | tf_op jit(solution)/shard_map/ppermute | solution.py:18
  87.2 0.9 collective-permute-done.6
  88.1 0.4 copy.56
  88.6 0.4 copy.57
  89.0 0.9 select_maximum_fusion
  90.0 0.5 fusion.27
  90.7 0.5 convolution_add_fusion.6
  91.2 0.5 convolution_add_fusion.5
  92.0 0.7 convolution_add_fusion.3
  93.0 0.5 convolution_add_fusion.1
  93.4 0.5 fusion.20
  94.0 0.6 copy.60
  94.6 19.2 %all_to_all.50 = f32[1,16,69,128]{3,0,2,1:T(1,128)S(1)} all-to-all(f32[1,16,69,128]{3,0,2,1:T(1,128)S(1)} %copy.60), channel_id=1, replica_groups=mesh['lvl'=8,'lon'=4] {'lvl'}, dimensions={1} | all-to-all | bytes 1130496 | tf_op jit(solution)/shard_map/all_to_all | solution.py:67
  114.5 18.8 %all_to_all.51 = f32[8,2,69,128]{3,1,2,0:T(2,128)S(1)} all-to-all(f32[8,2,69,128]{3,1,2,0:T(2,128)S(1)} %concatenate.55.clone), channel_id=1, replica_groups=mesh['lvl'=8,'lon'=4] {'lvl'}, dimensions={0} | all-to-all | bytes 1130496 | tf_op jit(solution)/shard_map/all_to_all | solution.py:69
  133.6 0.9 copy.64
  (49 shorter events, 4.3 us)
Async XLA Ops:
  0.0 4.6 %copy-start.9 = (s32[256]{0:T(256)S(1)}, s32[256]{0:T(256)}, u32[]{:S(2)}) copy-start(s32[256]{0:T(256)} %param.14) | copy-start | bytes 3076
  0.0 5.3 %copy-start.6 = (bf16[3,3,192,69]{2,3,1,0:T(8,128)(2,1)S(1)}, bf16[3,3,192,69]{2,3,1,0:T(8,128)(2,1)}, u32[]{:S(2)}) copy-start(bf16[3,3,192,69]{2,3,1,0:T(8,128)(2,1)} %param.11) | copy-start | bytes 715396
  1.3 5.1 %copy-start.8 = (f32[192]{0:T(256)S(1)}, f32[192]{0:T(256)}, u32[]{:S(2)}) copy-start(f32[192]{0:T(256)} %param.13) | copy-start | bytes 2308
  1.5 7.4 %collective-permute-start = (bf16[1,16,69,1]{3,2,1,0:T(8,128)(2,1)S(1)}, bf16[1,16,69,1]{3,2,1,0:T(8,128)(2,1)S(1)}, u32[]{:S(2)}, u32[]{:S(2)}) collective-permute-start(bf16[1,16,69,1]{3,2,1,0:T(8,128)(2,1)S(1)} %get-tuple-element.13), channel_id=1, source_target_pairs={{0,1},{1,2},{2,3},{3,0},{4,5},{5,6},{6,7},{7,4},{8,9},{9,10},{10,1... | collective-permute-start | bytes 6632 | tf_op jit(solution)/shard_map/ppermute | solution.py:15
  2.0 9.3 %collective-permute-start.1 = (bf16[1,16,69,1]{3,2,1,0:T(8,128)(2,1)S(1)}, bf16[1,16,69,1]{3,2,1,0:T(8,128)(2,1)S(1)}, u32[]{:S(2)}, u32[]{:S(2)}) collective-permute-start(bf16[1,16,69,1]{3,2,1,0:T(8,128)(2,1)S(1)} %get-tuple-element.14), channel_id=1, source_target_pairs={{1,0},{2,1},{3,2},{0,3},{5,4},{6,5},{7,6},{4,7},{9,8},{10,9},{11,1... | collective-permute-start | bytes 6632 | tf_op jit(solution)/shard_map/ppermute | solution.py:18
  16.8 4.8 %collective-permute-start.2 = (bf16[1,16,192,1]{2,1,3,0:T(8,128)(2,1)S(1)}, bf16[1,16,192,1]{2,1,3,0:T(8,128)(2,1)S(1)}, u32[]{:S(2)}, u32[]{:S(2)}) collective-permute-start(bf16[1,16,192,1]{2,1,3,0:T(8,128)(2,1)S(1)} %copy.42), channel_id=1, source_target_pairs={{0,1},{1,2},{2,3},{3,0},{4,5},{5,6},{6,7},{7,4},{8,9},{9,10},{10,1... | collective-permute-start | bytes 18440 | tf_op jit(solution)/shard_map/ppermute | solution.py:15
  17.2 4.8 %collective-permute-start.3 = (bf16[1,16,192,1]{2,1,3,0:T(8,128)(2,1)S(1)}, bf16[1,16,192,1]{2,1,3,0:T(8,128)(2,1)S(1)}, u32[]{:S(2)}, u32[]{:S(2)}) collective-permute-start(bf16[1,16,192,1]{2,1,3,0:T(8,128)(2,1)S(1)} %copy.43), channel_id=1, source_target_pairs={{1,0},{2,1},{3,2},{0,3},{5,4},{6,5},{7,6},{4,7},{9,8},{10,9},{11,1... | collective-permute-start | bytes 18440 | tf_op jit(solution)/shard_map/ppermute | solution.py:18
  22.5 1.0 copy-start.4
  26.2 1.1 copy-start
  26.2 1.2 copy-start.1
  51.2 19.0 %copy-start.2 = (f32[16,69,128]{2,0,1:T(8,128)S(1)}, f32[16,69,128]{2,0,1:T(8,128)}, u32[]{:S(2)}) copy-start(f32[16,69,128]{2,0,1:T(8,128)} %param.9) | copy-start | bytes 1695748
  70.3 2.2 %copy-start.7 = (bf16[3,3,192,69]{2,3,1,0:T(8,128)(2,1)S(1)}, bf16[3,3,192,69]{2,3,1,0:T(8,128)(2,1)}, u32[]{:S(2)}) copy-start(bf16[3,3,192,69]{2,3,1,0:T(8,128)(2,1)} %param.11) | copy-start | bytes 715396
  70.7 8.9 %collective-permute-start.4 = (bf16[1,16,69,1]{3,2,1,0:T(8,128)(2,1)S(1)}, bf16[1,16,69,1]{3,2,1,0:T(8,128)(2,1)S(1)}, u32[]{:S(2)}, u32[]{:S(2)}) collective-permute-start(bf16[1,16,69,1]{3,2,1,0:T(8,128)(2,1)S(1)} %get-tuple-element.11), channel_id=1, source_target_pairs={{0,1},{1,2},{2,3},{3,0},{4,5},{5,6},{6,7},{7,4},{8,9},{9,10},{10,1... | collective-permute-start | bytes 6632 | tf_op jit(solution)/shard_map/ppermute | solution.py:15
  70.7 8.8 %collective-permute-start.5 = (bf16[1,16,69,1]{3,2,1,0:T(8,128)(2,1)S(1)}, bf16[1,16,69,1]{3,2,1,0:T(8,128)(2,1)S(1)}, u32[]{:S(2)}, u32[]{:S(2)}) collective-permute-start(bf16[1,16,69,1]{3,2,1,0:T(8,128)(2,1)S(1)} %get-tuple-element.12), channel_id=1, source_target_pairs={{1,0},{2,1},{3,2},{0,3},{5,4},{6,5},{7,6},{4,7},{9,8},{10,9},{11,1... | collective-permute-start | bytes 6632 | tf_op jit(solution)/shard_map/ppermute | solution.py:18
  85.0 3.1 %collective-permute-start.6 = (bf16[1,16,192,1]{2,1,3,0:T(8,128)(2,1)S(1)}, bf16[1,16,192,1]{2,1,3,0:T(8,128)(2,1)S(1)}, u32[]{:S(2)}, u32[]{:S(2)}) collective-permute-start(bf16[1,16,192,1]{2,1,3,0:T(8,128)(2,1)S(1)} %copy.54), channel_id=1, source_target_pairs={{0,1},{1,2},{2,3},{3,0},{4,5},{5,6},{6,7},{7,4},{8,9},{9,10},{10,1... | collective-permute-start | bytes 18440 | tf_op jit(solution)/shard_map/ppermute | solution.py:15
  85.7 2.8 %collective-permute-start.7 = (bf16[1,16,192,1]{2,1,3,0:T(8,128)(2,1)S(1)}, bf16[1,16,192,1]{2,1,3,0:T(8,128)(2,1)S(1)}, u32[]{:S(2)}, u32[]{:S(2)}) collective-permute-start(bf16[1,16,192,1]{2,1,3,0:T(8,128)(2,1)S(1)} %copy.55), channel_id=1, source_target_pairs={{1,0},{2,1},{3,2},{0,3},{5,4},{6,5},{7,6},{4,7},{9,8},{10,9},{11,1... | collective-permute-start | bytes 18440 | tf_op jit(solution)/shard_map/ppermute | solution.py:18
  89.0 1.0 copy-start.5
  114.3 19.0 %copy-start.3 = (f32[16,69,128]{2,0,1:T(8,128)S(1)}, f32[16,69,128]{2,0,1:T(8,128)}, u32[]{:S(2)}) copy-start(f32[16,69,128]{2,0,1:T(8,128)} %param.9) | copy-start | bytes 1695748
where the time goes:
time: 135 us
  blocking collectives  78.9 us (58%)
  matrix products  17.5 us (13%)
  waiting for transfers between devices  12.5 us (9%)
  local copies, waits for them, and re-layouts  9.75 us (7%)
  starting transfers between devices  8.49 us (6%)
  between operations  3.93 us (3%)
  other arithmetic  3.51 us (3%)
    all_to_all x2, blocking collectives, body(): lax.all_to_all(increment, 'lvl', split_axis=1, concat_axis=0, tiled=True)  41.3 us
    all_to_all x2, blocking collectives, body(): lax.all_to_all(earlier, 'lvl', split_axis=0, concat_axis=1, tiled=True)  37.6 us
    dot_general x36, matrix products, convolve(): jnp.einsum('oc,vlcn->vlon', weight[a, b], piece, preferred_element_type=j...  17.5 us
    ppermute x4, waiting for transfers between devices, extended(): lax.ppermute(lax.slice_in_dim(block, block.shape[dim] - width, None, axis...  10 us
    ppermute x4, starting transfers between devices, extended(): lax.ppermute(lax.slice_in_dim(block, 0, width, axis=dim), axis, backward)  7.5 us
  transfers between devices with their start and end apart: 8, of which 4 were waited for; matrix products, arithmetic and copies ran while one was open for 2% of the time, Pallas kernels for 0%

commit v1 on v0

--- a/solution.py
+++ b/solution.py
@@ -64,7 +64,12 @@
         score = convolve(pad_rows(hidden_wide), conv_out, width)
         increment = (0.5 * beta_col * states + beta_col * score) * step_col + spread
         earlier = exclusive_sum(
-            lax.all_to_all(increment, "lvl", split_axis=1, concat_axis=0, tiled=True)
+            jnp.concatenate(
+                lax.all_to_all(
+                    jnp.stack(jnp.split(increment, lax.axis_size("lvl"), axis=1)), "lvl", 0, 0
+                ),
+                axis=0,
+            )
         )
         before = lax.all_to_all(earlier, "lvl", split_axis=0, concat_axis=1, tiled=True)
         inclusive = before + increment

time: 135 us -> 134 us (level)
  transfers between devices with their start and end apart: 8 -> 8, of which waited for: 4 -> 5; matrix products, arithmetic and copies ran while one was open for 2% -> 2% of each run, Pallas kernels for 0% -> 0%
where the time goes in v1:
time: 134 us
  blocking collectives  78.9 us (59%)
  matrix products  17.5 us (13%)
  waiting for transfers between devices  12.5 us (9%)
  local copies, waits for them, and re-layouts  8.81 us (7%)
  starting transfers between devices  8.53 us (6%)
  between operations  4.02 us (3%)
  other arithmetic  3.56 us (3%)
    all_to_all x2, blocking collectives, body(): lax.all_to_all(jnp.stack(jnp.split(increment, lax.axis_size('lvl'), axis=...  41.3 us
    all_to_all x2, blocking collectives, body(): lax.all_to_all(earlier, 'lvl', split_axis=0, concat_axis=1, tiled=True)  37.6 us
    dot_general x36, matrix products, convolve(): jnp.einsum('oc,vlcn->vlon', weight[a, b], piece, preferred_element_type=j...  17.5 us
    ppermute x4, waiting for transfers between devices, extended(): lax.ppermute(lax.slice_in_dim(block, block.shape[dim] - width, None, axis...  9.83 us
    ppermute x4, starting transfers between devices, extended(): lax.ppermute(lax.slice_in_dim(block, 0, width, axis=dim), axis, backward)  7.54 us
  transfers between devices with their start and end apart: 8, of which 5 were waited for; matrix products, arithmetic and copies ran while one was open for 2% of the time, Pallas kernels for 0%

profile of v1, /device:TPU:0, one launch (start us, length us, event | category | flops | bytes accessed | tf_op | source)
XLA Modules:
  0.0 133.8 jit_solution(5981259884612654695)
XLA Ops:
  0.0 1.3 copy.46
  1.5 0.5 collective-permute-start
  2.0 2.0 %collective-permute-start.1 = (bf16[1,16,69,1]{3,2,1,0:T(8,128)(2,1)S(1)}, bf16[1,16,69,1]{3,2,1,0:T(8,128)(2,1)S(1)}, u32[]{:S(2)}, u32[]{:S(2)}) collective-permute-start(bf16[1,16,69,1]{3,2,1,0:T(8,128)(2,1)S(1)} %get-tuple-element.14), channel_id=1, source_target_pairs={{1,0},{2,1},{3,2},{0,3},{5,4},{6,5},{7,6},{4,7},{9,8},{10,9},{11,1... | collective-permute-start | bytes 6632 | tf_op jit(solution)/shard_map/ppermute | solution.py:18
  4.7 0.6 fusion.173
  5.3 0.4 fusion.69
  6.4 2.4 %collective-permute-done = bf16[1,16,69,1]{3,2,1,0:T(8,128)(2,1)S(1)} collective-permute-done((bf16[1,16,69,1]{3,2,1,0:T(8,128)(2,1)S(1)}, bf16[1,16,69,1]{3,2,1,0:T(8,128)(2,1)S(1)}, u32[]{:S(2)}, u32[]{:S(2)}) %collective-permute-start) | collective-permute-done | bytes 2240 | tf_op jit(solution)/shard_map/ppermute | solution.py:15
  8.9 2.4 %collective-permute-done.1 = bf16[1,16,69,1]{3,2,1,0:T(8,128)(2,1)S(1)} collective-permute-done((bf16[1,16,69,1]{3,2,1,0:T(8,128)(2,1)S(1)}, bf16[1,16,69,1]{3,2,1,0:T(8,128)(2,1)S(1)}, u32[]{:S(2)}, u32[]{:S(2)}) %collective-permute-start.1) | collective-permute-done | bytes 2240 | tf_op jit(solution)/shard_map/ppermute | solution.py:18
  11.3 0.4 select_maximum_fusion.6
  11.7 0.5 fusion.57
  12.2 0.4 fusion.58
  12.6 0.5 fusion.66
  13.0 0.5 fusion.67
  13.5 0.4 fusion.68
  13.9 0.5 fusion.56
  14.4 0.5 fusion.63
  14.9 1.2 fusion.8
  16.1 0.3 fusion.170
  16.4 0.4 copy.18
  16.8 0.4 copy.19
  17.2 2.1 %collective-permute-start.3 = (bf16[1,16,192,1]{2,1,3,0:T(8,128)(2,1)S(1)}, bf16[1,16,192,1]{2,1,3,0:T(8,128)(2,1)S(1)}, u32[]{:S(2)}, u32[]{:S(2)}) collective-permute-start(bf16[1,16,192,1]{2,1,3,0:T(8,128)(2,1)S(1)} %copy.19), channel_id=1, source_target_pairs={{1,0},{2,1},{3,2},{0,3},{5,4},{6,5},{7,6},{4,7},{9,8},{10,9},{11,1... | collective-permute-start | bytes 18440 | tf_op jit(solution)/shard_map/ppermute | solution.py:18
  21.4 0.4 copy.20
  21.9 0.4 copy.21
  22.3 0.9 select_maximum_fusion.2
  23.3 0.5 fusion.34
  24.0 0.5 convolution_add_fusion.14
  24.5 0.5 convolution_add_fusion.13
  25.3 0.7 convolution_add_fusion.11
  26.3 0.5 convolution_add_fusion.9
  26.7 0.3 copy-done
  27.2 0.6 fusion.17
  28.0 0.3 copy.25
  28.3 22.1 %all_to_all.34 = f32[8,1,2,69,128]{4,2,3,1,0:T(2,128)S(1)} all-to-all(f32[8,1,2,69,128]{4,2,3,1,0:T(2,128)S(1)} %copy.25), channel_id=1, replica_groups=mesh['lvl'=8,'lon'=4] {'lvl'}, dimensions={0} | all-to-all | bytes 1130496 | tf_op jit(solution)/shard_map/all_to_all | solution.py:68
  50.9 18.8 %all_to_all.35 = f32[8,2,69,128]{3,1,2,0:T(2,128)S(1)} all-to-all(f32[8,2,69,128]{3,1,2,0:T(2,128)S(1)} %concatenate.48), channel_id=1, replica_groups=mesh['lvl'=8,'lon'=4] {'lvl'}, dimensions={0} | all-to-all | bytes 1130496 | tf_op jit(solution)/shard_map/all_to_all | solution.py:74
  70.1 1.7 %collective-permute-start.5 = (bf16[1,16,69,1]{3,2,1,0:T(8,128)(2,1)S(1)}, bf16[1,16,69,1]{3,2,1,0:T(8,128)(2,1)S(1)}, u32[]{:S(2)}, u32[]{:S(2)}) collective-permute-start(bf16[1,16,69,1]{3,2,1,0:T(8,128)(2,1)S(1)} %get-tuple-element.12), channel_id=1, source_target_pairs={{1,0},{2,1},{3,2},{0,3},{5,4},{6,5},{7,6},{4,7},{9,8},{10,9},{11,1... | collective-permute-start | bytes 6632 | tf_op jit(solution)/shard_map/ppermute | solution.py:18
  71.9 0.4 fusion.71
  72.3 6.7 %collective-permute-done.4 = bf16[1,16,69,1]{3,2,1,0:T(8,128)(2,1)S(1)} collective-permute-done((bf16[1,16,69,1]{3,2,1,0:T(8,128)(2,1)S(1)}, bf16[1,16,69,1]{3,2,1,0:T(8,128)(2,1)S(1)}, u32[]{:S(2)}, u32[]{:S(2)}) %collective-permute-start.4) | collective-permute-done | bytes 2240 | tf_op jit(solution)/shard_map/ppermute | solution.py:15
  79.0 0.4 select_maximum_fusion.4
  79.3 0.5 fusion.44
  79.8 0.4 fusion.45
  80.2 0.5 fusion.53
  80.7 0.5 fusion.54
  81.2 0.4 fusion.55
  81.6 0.5 fusion.43
  82.1 0.5 fusion.50
  82.5 1.2 fusion.9
  83.7 0.3 fusion.169
  84.1 0.4 copy.28
  84.4 0.3 collective-permute-start.6
  84.8 0.4 copy.29
  85.1 1.7 %collective-permute-start.7 = (bf16[1,16,192,1]{2,1,3,0:T(8,128)(2,1)S(1)}, bf16[1,16,192,1]{2,1,3,0:T(8,128)(2,1)S(1)}, u32[]{:S(2)}, u32[]{:S(2)}) collective-permute-start(bf16[1,16,192,1]{2,1,3,0:T(8,128)(2,1)S(1)} %copy.29), channel_id=1, source_target_pairs={{1,0},{2,1},{3,2},{0,3},{5,4},{6,5},{7,6},{4,7},{9,8},{10,9},{11,1... | collective-permute-start | bytes 18440 | tf_op jit(solution)/shard_map/ppermute | solution.py:18
  86.8 0.7 collective-permute-done.6
  87.5 0.4 copy.30
  88.2 0.4 copy.31
  88.7 0.9 select_maximum_fusion
  89.6 0.5 fusion.27
  90.4 0.5 convolution_add_fusion.6
  90.8 0.5 convolution_add_fusion.5
  91.6 0.7 convolution_add_fusion.3
  92.6 0.5 convolution_add_fusion.1
  93.1 0.5 fusion.20
  93.8 0.3 copy.34
  94.1 19.2 %all_to_all.36 = f32[8,1,2,69,128]{4,2,3,1,0:T(2,128)S(1)} all-to-all(f32[8,1,2,69,128]{4,2,3,1,0:T(2,128)S(1)} %copy.34), channel_id=1, replica_groups=mesh['lvl'=8,'lon'=4] {'lvl'}, dimensions={0} | all-to-all | bytes 1130496 | tf_op jit(solution)/shard_map/all_to_all | solution.py:68
  113.8 18.8 %all_to_all.37 = f32[8,2,69,128]{3,1,2,0:T(2,128)S(1)} all-to-all(f32[8,2,69,128]{3,1,2,0:T(2,128)S(1)} %concatenate.55), channel_id=1, replica_groups=mesh['lvl'=8,'lon'=4] {'lvl'}, dimensions={0} | all-to-all | bytes 1130496 | tf_op jit(solution)/shard_map/all_to_all | solution.py:74
  132.9 0.9 copy.36
  (61 shorter events, 4.2 us)
Async XLA Ops:
  0.0 4.6 %copy-start.9 = (s32[256]{0:T(256)S(1)}, s32[256]{0:T(256)}, u32[]{:S(2)}) copy-start(s32[256]{0:T(256)} %param.14) | copy-start | bytes 3076
  0.0 5.3 %copy-start.6 = (bf16[3,3,192,69]{2,3,1,0:T(8,128)(2,1)S(1)}, bf16[3,3,192,69]{2,3,1,0:T(8,128)(2,1)}, u32[]{:S(2)}) copy-start(bf16[3,3,192,69]{2,3,1,0:T(8,128)(2,1)} %param.11) | copy-start | bytes 715396
  1.3 5.1 %copy-start.8 = (f32[192]{0:T(256)S(1)}, f32[192]{0:T(256)}, u32[]{:S(2)}) copy-start(f32[192]{0:T(256)} %param.13) | copy-start | bytes 2308
  1.5 7.4 %collective-permute-start = (bf16[1,16,69,1]{3,2,1,0:T(8,128)(2,1)S(1)}, bf16[1,16,69,1]{3,2,1,0:T(8,128)(2,1)S(1)}, u32[]{:S(2)}, u32[]{:S(2)}) collective-permute-start(bf16[1,16,69,1]{3,2,1,0:T(8,128)(2,1)S(1)} %get-tuple-element.13), channel_id=1, source_target_pairs={{0,1},{1,2},{2,3},{3,0},{4,5},{5,6},{6,7},{7,4},{8,9},{9,10},{10,1... | collective-permute-start | bytes 6632 | tf_op jit(solution)/shard_map/ppermute | solution.py:15
  2.0 9.3 %collective-permute-start.1 = (bf16[1,16,69,1]{3,2,1,0:T(8,128)(2,1)S(1)}, bf16[1,16,69,1]{3,2,1,0:T(8,128)(2,1)S(1)}, u32[]{:S(2)}, u32[]{:S(2)}) collective-permute-start(bf16[1,16,69,1]{3,2,1,0:T(8,128)(2,1)S(1)} %get-tuple-element.14), channel_id=1, source_target_pairs={{1,0},{2,1},{3,2},{0,3},{5,4},{6,5},{7,6},{4,7},{9,8},{10,9},{11,1... | collective-permute-start | bytes 6632 | tf_op jit(solution)/shard_map/ppermute | solution.py:18
  16.8 4.6 %collective-permute-start.2 = (bf16[1,16,192,1]{2,1,3,0:T(8,128)(2,1)S(1)}, bf16[1,16,192,1]{2,1,3,0:T(8,128)(2,1)S(1)}, u32[]{:S(2)}, u32[]{:S(2)}) collective-permute-start(bf16[1,16,192,1]{2,1,3,0:T(8,128)(2,1)S(1)} %copy.18), channel_id=1, source_target_pairs={{0,1},{1,2},{2,3},{3,0},{4,5},{5,6},{6,7},{7,4},{8,9},{9,10},{10,1... | collective-permute-start | bytes 18440 | tf_op jit(solution)/shard_map/ppermute | solution.py:15
  17.2 4.6 %collective-permute-start.3 = (bf16[1,16,192,1]{2,1,3,0:T(8,128)(2,1)S(1)}, bf16[1,16,192,1]{2,1,3,0:T(8,128)(2,1)S(1)}, u32[]{:S(2)}, u32[]{:S(2)}) collective-permute-start(bf16[1,16,192,1]{2,1,3,0:T(8,128)(2,1)S(1)} %copy.19), channel_id=1, source_target_pairs={{1,0},{2,1},{3,2},{0,3},{5,4},{6,5},{7,6},{4,7},{9,8},{10,9},{11,1... | collective-permute-start | bytes 18440 | tf_op jit(solution)/shard_map/ppermute | solution.py:18
  22.3 1.0 copy-start.4
  26.0 1.1 copy-start
  26.0 1.2 copy-start.1
  50.7 19.0 %copy-start.2 = (f32[16,69,128]{2,0,1:T(8,128)S(1)}, f32[16,69,128]{2,0,1:T(8,128)}, u32[]{:S(2)}) copy-start(f32[16,69,128]{2,0,1:T(8,128)} %param.9) | copy-start | bytes 1695748
  69.7 2.2 %copy-start.7 = (bf16[3,3,192,69]{2,3,1,0:T(8,128)(2,1)S(1)}, bf16[3,3,192,69]{2,3,1,0:T(8,128)(2,1)}, u32[]{:S(2)}) copy-start(bf16[3,3,192,69]{2,3,1,0:T(8,128)(2,1)} %param.11) | copy-start | bytes 715396
  70.1 8.9 %collective-permute-start.4 = (bf16[1,16,69,1]{3,2,1,0:T(8,128)(2,1)S(1)}, bf16[1,16,69,1]{3,2,1,0:T(8,128)(2,1)S(1)}, u32[]{:S(2)}, u32[]{:S(2)}) collective-permute-start(bf16[1,16,69,1]{3,2,1,0:T(8,128)(2,1)S(1)} %get-tuple-element.11), channel_id=1, source_target_pairs={{0,1},{1,2},{2,3},{3,0},{4,5},{5,6},{6,7},{7,4},{8,9},{9,10},{10,1... | collective-permute-start | bytes 6632 | tf_op jit(solution)/shard_map/ppermute | solution.py:15
  70.1 8.8 %collective-permute-start.5 = (bf16[1,16,69,1]{3,2,1,0:T(8,128)(2,1)S(1)}, bf16[1,16,69,1]{3,2,1,0:T(8,128)(2,1)S(1)}, u32[]{:S(2)}, u32[]{:S(2)}) collective-permute-start(bf16[1,16,69,1]{3,2,1,0:T(8,128)(2,1)S(1)} %get-tuple-element.12), channel_id=1, source_target_pairs={{1,0},{2,1},{3,2},{0,3},{5,4},{6,5},{7,6},{4,7},{9,8},{10,9},{11,1... | collective-permute-start | bytes 6632 | tf_op jit(solution)/shard_map/ppermute | solution.py:18
  84.4 3.1 %collective-permute-start.6 = (bf16[1,16,192,1]{2,1,3,0:T(8,128)(2,1)S(1)}, bf16[1,16,192,1]{2,1,3,0:T(8,128)(2,1)S(1)}, u32[]{:S(2)}, u32[]{:S(2)}) collective-permute-start(bf16[1,16,192,1]{2,1,3,0:T(8,128)(2,1)S(1)} %copy.28), channel_id=1, source_target_pairs={{0,1},{1,2},{2,3},{3,0},{4,5},{5,6},{6,7},{7,4},{8,9},{9,10},{10,1... | collective-permute-start | bytes 18440 | tf_op jit(solution)/shard_map/ppermute | solution.py:15
  85.1 3.1 %collective-permute-start.7 = (bf16[1,16,192,1]{2,1,3,0:T(8,128)(2,1)S(1)}, bf16[1,16,192,1]{2,1,3,0:T(8,128)(2,1)S(1)}, u32[]{:S(2)}, u32[]{:S(2)}) collective-permute-start(bf16[1,16,192,1]{2,1,3,0:T(8,128)(2,1)S(1)} %copy.29), channel_id=1, source_target_pairs={{1,0},{2,1},{3,2},{0,3},{5,4},{6,5},{7,6},{4,7},{9,8},{10,9},{11,1... | collective-permute-start | bytes 18440 | tf_op jit(solution)/shard_map/ppermute | solution.py:18
  88.6 1.0 copy-start.5
  113.5 19.0 %copy-start.3 = (f32[16,69,128]{2,0,1:T(8,128)S(1)}, f32[16,69,128]{2,0,1:T(8,128)}, u32[]{:S(2)}) copy-start(f32[16,69,128]{2,0,1:T(8,128)} %param.9) | copy-start | bytes 1695748
